TPU v7x, 32 devices: a 4x4x1 block of a 4x4x8 slice. The times are simulated.
32 devices in a mesh: dp: 2 (over z, core), tp: 16 (over x, y).
Axes of the slice: x: 4, y: 4, z: 1, core: 2. Of those that a mesh axis runs over, the one named last changes fastest.
The devices are a block of a 4x4x8 slice.
Arguments:
- x: bfloat16 [256, 8192], P('dp'), parts along dimension 0
- w_gate: bfloat16 [8192, 32768], P(None, 'tp')
- w_up: bfloat16 [8192, 32768], P(None, 'tp')
- w_down: bfloat16 [32768, 8192], P('tp')
Outputs:
- output: bfloat16 [256, 8192], P('dp'), parts along dimension 0
There are 2 independent parts. A program takes and returns all parts, laid end to end along the dimension named above; an argument that names none is the same for every part.
All inputs are finite; a program needn't handle non-finite values.
Results may differ from a plain program's by a relative error of at most 0.016.
Values are sent between devices in bfloat16 or wider.
A program may use at most 768 MiB of HBM per device.

v0:
```python
import jax
import jax.numpy as jnp
from jax import lax
from jax.sharding import PartitionSpec as P


def solution(mesh):
    def step(x, w_gate, w_up, w_down):
        gate = jnp.dot(x, w_gate, preferred_element_type=jnp.float32)
        up = jnp.dot(x, w_up, preferred_element_type=jnp.float32)
        hidden = (jax.nn.silu(gate) * up).astype(jnp.bfloat16)
        term = jnp.dot(hidden, w_down, preferred_element_type=jnp.float32).astype(jnp.bfloat16)
        return lax.psum(term, "tp")

    return jax.shard_map(
        step,
        mesh=mesh,
        in_specs=(P("dp", None), P(None, "tp"), P(None, "tp"), P("tp", None)),
        out_specs=P("dp", None),
        check_vma=False,
    )
```

profile of v0, /device:TPU:96, one launch (start us, length us, event | category | flops | bytes accessed | tf_op | source)
XLA Modules:
  0.0 138.6 jit_solution(17045647911711162599)
XLA Ops:
  6.5 0.0 copy-start
  6.6 0.0 all-reduce.2.cloned.1.call-start
  6.6 1.6 %copy-done = bf16[128,8192]{1,0:T(8,128)(2,1)S(1)} copy-done((bf16[128,8192]{1,0:T(8,128)(2,1)S(1)}, bf16[128,8192]{1,0:T(8,128)(2,1)}, u32[]{:S(2)}) %copy-start) | copy-done | bytes 2097176
  8.1 12.9 %fusion.8 = f32[128,2048]{1,0:T(8,128)S(1)} fusion(bf16[128,8192]{1,0:T(8,128)(2,1)S(1)} %copy-done, bf16[8192,2048]{1,0:T(8,128)(2,1)} %param.5), kind=kOutput, calls=%fused_computation.10 | convolution fusion | flops 4294967296 | bytes 36700160 | tf_op jit(solution)/shard_map/dot_general | solution.py:9
  21.0 24.5 %convolution_convert_fusion = bf16[128,8192]{1,0:T(8,128)(2,1)} fusion(bf16[2048,8192]{1,0:T(8,128)(2,1)} %param.7, bf16[128,8192]{1,0:T(8,128)(2,1)S(1)} %copy-done, bf16[8192,2048]{1,0:T(8,128)(2,1)} %param.6, f32[128,2048]{1,0:T(8,128)S(1)} %fusion.8), kind=kOutput, calls=%fused_computation | convolution fusion | flops 8592556032 | bytes 72351744 | tf_op jit(solution)/shard_map/dot_general | solution.py:12
  45.5 0.1 all-reduce.2.cloned.1.call-update
  45.6 83.1 %all-reduce.2.cloned.1.call-done = bf16[128,8192]{1,0:T(8,128)(2,1)} async-done(((bf16[128,8192]{1,0:T(8,128)(2,1)}), bf16[128,8192]{1,0:T(8,128)(2,1)}) %all-reduce.2.cloned.1.call-update) | async-done | bytes 2097168 | tf_op jit(solution)/shard_map/psum | solution.py:13
  128.7 3.1 %copy.6 = bf16[128,8192]{1,0:T(8,128)(2,1)} copy(bf16[128,8192]{1,0:T(8,128)(2,1)} %all-reduce.2.cloned.1.call-done) | data formatting | bytes 4194304
Async XLA Ops:
  6.5 1.6 %copy-start = (bf16[128,8192]{1,0:T(8,128)(2,1)S(1)}, bf16[128,8192]{1,0:T(8,128)(2,1)}, u32[]{:S(2)}) copy-start(bf16[128,8192]{1,0:T(8,128)(2,1)} %param.4) | copy-start | bytes 6291460
  6.6 122.1 %all-reduce.2.cloned.1.call-start = ((), (), s32[]{:S(2)}) async-start(), calls=%async_computation | async-start | bytes 4194304 | tf_op jit(solution)/shard_map/psum | solution.py:13
Sparse Core Ops, SparseCore 0:
  45.7 82.9 all-reduce.1
where the time goes:
time: 139 us
  waiting for transfers between devices  83.1 us (60%)
  matrix products  37.4 us (27%)
  between operations  13.4 us (10%)
  local copies, waits for them, and re-layouts  4.68 us (3%)
    psum x1, waiting for transfers between devices, step(): return lax.psum(term, 'tp')  83.1 us
    dot_general x1, matrix products, step(): jnp.dot(hidden, w_down, preferred_element_type=jnp.float32)  24.5 us
    dot_general x1, matrix products, step(): gate = jnp.dot(x, w_gate, preferred_element_type=jnp.float32)  12.9 us
    unnamed x3, local copies, waits for them, and re-layouts  4.68 us
  transfers between devices with their start and end apart: 1, of which 1 were waited for; matrix products, arithmetic and copies ran while one was open for 0% of the time, Pallas kernels for 0%

commit v1 on v0

v1 whole, which is shorter than its diff:
```python
import functools
import math

import jax
import jax.numpy as jnp
from jax import lax
from jax.experimental import pallas as pl
from jax.experimental.pallas import tpu as pltpu
from jax.sharding import PartitionSpec as P

MESH = pl.DeviceIdType.MESH
F32, BF16 = jnp.float32, jnp.bfloat16

KC = 1024
JC = 512
CW = 512
SLOTS = 8
LAG = 3


def kernel(
    side, x_ref, wg_ref, wu_ref, wd_ref, out_ref,
    xs, wgb, wub, wdb, accg, accu, hid, term, termb, r1, f1, red, redb, r2, f2, swp, ybuf,
    x_in, x_out, x_recv, w_in, wd_in, h_out, h_recv, y_out,
    s_r1, s_f1, s_r2, s_f2, s_sw, s_g1, s_g1f, s_g2, s_g2f,
    q_r1, q_f1, q_r2, q_f2, q_sw, q_g1, q_g2,
):
    rows, depth = x_ref.shape
    hw = wg_ref.shape[1] // 2
    cols = out_ref.shape[1] // 2
    nk, nj, nc = depth // KC, hw // JC, cols // CW
    nblk = nk * nj
    ow = CW // 2
    br, qr, qc = rows // side, rows // side // 2, ow // 2

    dp, tp = lax.axis_index("dp"), lax.axis_index("tp")
    h = lax.rem(dp, 2)
    other = 1 - h
    partner = (dp + 1 - 2 * h, tp)
    cx, cy = tp // side, lax.rem(tp, side)

    def near(axis, d):
        if axis == 0:
            return (dp, lax.rem(cx + d + side, side) * side + cy)
        return (dp, cx * side + lax.rem(cy + d + side, side))

    nbr = [[near(axis, 1), near(axis, -1)] for axis in (0, 1)]
    coord = [cx, cy]

    def send(src, dst, s_sem, r_sem, dev):
        return pltpu.make_async_remote_copy(
            src_ref=src, dst_ref=dst, send_sem=s_sem, recv_sem=r_sem, device_id=dev, device_id_type=MESH
        )

    def landed(dst, r_sem):
        pltpu.make_async_remote_copy(
            src_ref=dst, dst_ref=dst, send_sem=s_sw, recv_sem=r_sem, device_id=partner, device_id_type=MESH
        ).wait_recv()

    def left_device(ref, s_sem):
        pltpu.make_async_remote_copy(
            src_ref=ref, dst_ref=ref, send_sem=s_sem, recv_sem=s_sem, device_id=partner, device_id_type=MESH
        ).wait_send()

    def x_piece(k):
        c = pl.ds(k * KC, KC)
        return pltpu.make_async_copy(x_ref.at[:, c], xs.at[h, :, c], x_in.at[k])

    def w_block(i):
        j, k, slot = i // nk, lax.rem(i, nk), lax.rem(i, SLOTS)
        r = pl.ds(pl.multiple_of(k * KC, KC), KC)
        c = pl.ds(pl.multiple_of(h * hw + j * JC, JC), JC)
        return (
            pltpu.make_async_copy(wg_ref.at[r, c], wgb.at[slot], w_in.at[slot, 0]),
            pltpu.make_async_copy(wu_ref.at[r, c], wub.at[slot], w_in.at[slot, 1]),
        )

    def wd_block(c):
        cc = pl.ds(pl.multiple_of(h * cols + c * CW, CW), CW)
        return pltpu.make_async_copy(wd_ref.at[:, cc], wdb.at[c], wd_in.at[c])

    for k in range(nk):
        x_piece(k).start()
    for i in range(SLOTS):
        for cp in w_block(i):
            cp.start()

    barrier = pltpu.get_barrier_semaphore()
    for dev in (partner, *nbr[0], *nbr[1]):
        pl.semaphore_signal(barrier, inc=1, device_id=dev, device_id_type=MESH)
    pl.semaphore_wait(barrier, 5)

    for k in range(nk):
        x_piece(k).wait()
        c = pl.ds(k * KC, KC)
        send(xs.at[h, :, c], xs.at[h, :, c], x_out, x_recv.at[k], partner).start()

    for j in range(nj):
        accg[...] = jnp.zeros_like(accg)
        accu[...] = jnp.zeros_like(accu)

        def block(k, carry, j=j):
            i = j * nk + k
            slot = lax.rem(i, SLOTS)
            kc = pl.ds(pl.multiple_of(k * KC, KC), KC)
            if j == 0:
                landed(xs.at[other, :, kc], x_recv.at[k])
            for cp in w_block(i):
                cp.wait()
            lhs = xs[:, :, kc].reshape(2 * rows, KC)
            accg[...] += jnp.dot(lhs, wgb[slot], preferred_element_type=F32)
            accu[...] += jnp.dot(lhs, wub[slot], preferred_element_type=F32)

            @pl.when(i + SLOTS < nblk)
            def _():
                for cp in w_block(i + SLOTS):
                    cp.start()

            @pl.when((i + SLOTS >= nblk) & (i + SLOTS < nblk + nc))
            def _():
                wd_block(i + SLOTS - nblk).start()

            return carry

        lax.fori_loop(0, nk, block, 0)
        g = accg[...]
        hc = pl.ds(pl.multiple_of(h * hw + j * JC, JC), JC)
        hid[:, hc] = (jax.nn.silu(g) * accu[...]).astype(BF16)
        send(hid.at[:, hc], hid.at[:, hc], h_out, h_recv.at[j], partner).start()
    for c in range(SLOTS, nc):
        wd_block(c).start()
    for j in range(nj):
        hc = pl.ds(pl.multiple_of(other * hw + j * JC, JC), JC)
        landed(hid.at[:, hc], h_recv.at[j])

    def wrap(v):
        return lax.rem(v + 2 * side, side)

    def piece(c, o, b):
        a = coord[o]
        r = pl.ds(pl.multiple_of(a * br + (b // 2) * qr, qr), qr)
        q = pl.ds(pl.multiple_of(c * CW + o * ow + lax.rem(b, 2) * qc, qc), qc)
        return r, q

    def slab(c, o, a):
        r = pl.ds(pl.multiple_of(a * br, br), br)
        q = pl.ds(pl.multiple_of(c * CW + o * ow, ow), ow)
        return r, q

    def scatter_start(src, relay, fin, s_relay, s_fin, q_relay, q_fin, pos, dev):
        send(src.at[wrap(pos + 2), 0], relay.at[0], s_relay, q_relay.at[0], dev[0]).start()
        send(src.at[wrap(pos + 2), 1], relay.at[1], s_relay, q_relay.at[1], dev[1]).start()
        send(src.at[wrap(pos + 1), 1], fin.at[0, 1], s_fin, q_fin.at[0, 1], dev[0]).start()
        send(src.at[wrap(pos - 1), 0], fin.at[1, 0], s_fin, q_fin.at[1, 0], dev[1]).start()

    def scatter_relay(own, relay, fin, s_fin, q_relay, q_fin, pos, dev):
        for d in (0, 1):
            landed(relay.at[d], q_relay.at[d])
            q = wrap(pos + 1 - 2 * d)
            relay[d] = (relay[d].astype(F32) + own[q, d]).astype(BF16)
            send(relay.at[d], fin.at[d, d], s_fin, q_fin.at[d, d], dev[d]).start()

    def scatter_wait(fin, q_fin):
        for d in (0, 1):
            for g in (0, 1):
                landed(fin.at[d, g], q_fin.at[d, g])

    def make_term(c):
        wd_block(c).wait()
        t = jnp.dot(hid[...], wdb[c], preferred_element_type=F32)
        for o in (0, 1):
            for q in range(side):
                for g in (0, 1):
                    v = t[g * rows + q * br:g * rows + (q + 1) * br, o * ow:(o + 1) * ow]
                    term[c, o, q, g] = v
                    termb[c, o, q, g] = v.astype(BF16)
        for o in (0, 1):
            scatter_start(
                termb.at[c, o], r1.at[c, o], f1.at[c, o], s_r1, s_f1, q_r1.at[c, o], q_f1.at[c, o], coord[o], nbr[o]
            )

    def relay_1(c):
        for o in (0, 1):
            scatter_relay(
                term.at[c, o], r1.at[c, o], f1.at[c, o], s_f1, q_r1.at[c, o], q_f1.at[c, o], coord[o], nbr[o]
            )

    def reduce_1(c):
        for o in (0, 1):
            scatter_wait(f1.at[c, o], q_f1.at[c, o])
            for g in (0, 1):
                v = term[c, o, coord[o], g] + f1[c, o, 0, g].astype(F32) + f1[c, o, 1, g].astype(F32)
                for q in range(side):
                    w = v[(q // 2) * qr:(q // 2 + 1) * qr, (q % 2) * qc:(q % 2 + 1) * qc]
                    red[c, o, q, g] = w
                    redb[c, o, q, g] = w.astype(BF16)
            scatter_start(
                redb.at[c, o], r2.at[c, o], f2.at[c, o], s_r2, s_f2, q_r2.at[c, o], q_f2.at[c, o],
                coord[1 - o], nbr[1 - o],
            )

    def relay_2(c):
        for o in (0, 1):
            scatter_relay(
                red.at[c, o], r2.at[c, o], f2.at[c, o], s_f2, q_r2.at[c, o], q_f2.at[c, o], coord[1 - o], nbr[1 - o]
            )

    def reduce_2(c):
        for o in (0, 1):
            scatter_wait(f2.at[c, o], q_f2.at[c, o])
            b = coord[1 - o]

            def total(g):
                v = red[c, o, b, g] + f2[c, o, 0, g].astype(F32) + f2[c, o, 1, g].astype(F32)
                return v.astype(BF16)

            r, q = piece(c, o, b)
            swp[c, o] = total(other)
            send(swp.at[c, o], ybuf.at[h, r, q], s_sw, q_sw.at[c, o], partner).start()
            ybuf[h, r, q] = total(h)

    def gather_1(c):
        for o in (0, 1):
            r, q = piece(c, o, coord[1 - o])
            landed(ybuf.at[other, r, q], q_sw.at[c, o])
            for d in (0, 1):
                send(ybuf.at[:, r, q], ybuf.at[:, r, q], s_g1, q_g1.at[c, o, 0, d], nbr[1 - o][d]).start()

    def forward_1(c):
        for o in (0, 1):
            for d in (0, 1):
                r, q = piece(c, o, wrap(coord[1 - o] - 1 + 2 * d))
                landed(ybuf.at[:, r, q], q_g1.at[c, o, 0, d])
                send(ybuf.at[d, r, q], ybuf.at[d, r, q], s_g1f, q_g1.at[c, o, 1, d], nbr[1 - o][d]).start()

    def gather_2(c):
        for o in (0, 1):
            r, q = piece(c, o, wrap(coord[1 - o] + 2))
            for d in (0, 1):
                landed(ybuf.at[d, r, q], q_g1.at[c, o, 1, d])
            r, q = slab(c, o, coord[o])
            for d in (0, 1):
                send(ybuf.at[:, r, q], ybuf.at[:, r, q], s_g2, q_g2.at[c, o, 0, d], nbr[o][d]).start()

    def forward_2(c):
        for o in (0, 1):
            for d in (0, 1):
                r, q = slab(c, o, wrap(coord[o] - 1 + 2 * d))
                landed(ybuf.at[:, r, q], q_g2.at[c, o, 0, d])
                send(ybuf.at[d, r, q], ybuf.at[d, r, q], s_g2f, q_g2.at[c, o, 1, d], nbr[o][d]).start()

    def finish(c):
        for o in (0, 1):
            r, q = slab(c, o, wrap(coord[o] + 2))
            for d in (0, 1):
                landed(ybuf.at[d, r, q], q_g2.at[c, o, 1, d])
        for d in (0, 1):
            pltpu.make_async_copy(
                ybuf.at[d, :, pl.ds(pl.multiple_of(c * CW, CW), CW)],
                out_ref.at[:, pl.ds(pl.multiple_of(d * cols + c * CW, CW), CW)],
                y_out,
            ).start()

    stages = (
        make_term, relay_1, reduce_1, relay_2, reduce_2, gather_1, forward_1, gather_2, forward_2, finish,
    )

    def tick(t, carry):
        for s, stage in enumerate(stages):
            c = t - s * LAG

            @pl.when((c >= 0) & (c < nc))
            def _(stage=stage, c=c):
                stage(c)

        return carry

    lax.fori_loop(0, nc + (len(stages) - 1) * LAG, tick, 0)

    left_device(ybuf, x_out)
    left_device(hid.at[:, pl.ds(0, hw)], h_out)
    left_device(r1, s_r1)
    left_device(f1, s_f1)
    left_device(r2, s_r2)
    left_device(f2, s_f2)
    left_device(swp, s_sw)
    left_device(f2, s_g1)
    left_device(r2, s_g1f)
    left_device(f1, s_g2)
    left_device(r1, s_g2f)
    pltpu.make_async_copy(ybuf, ybuf, y_out).wait()


def solution(mesh):
    side = math.isqrt(mesh.shape["tp"])

    def step(x, w_gate, w_up, w_down):
        rows, depth = x.shape
        hw = w_gate.shape[1] // 2
        cols = w_down.shape[1] // 2
        nk, nj, nc = depth // KC, hw // JC, cols // CW
        ow = CW // 2
        br, qr, qc = rows // side, rows // side // 2, ow // 2
        dma = pltpu.SemaphoreType.DMA
        scratch = [
            pltpu.VMEM((2, rows, depth), BF16),
            pltpu.VMEM((SLOTS, KC, JC), BF16),
            pltpu.VMEM((SLOTS, KC, JC), BF16),
            pltpu.VMEM((nc, 2 * hw, CW), BF16),
            pltpu.VMEM((2 * rows, JC), F32),
            pltpu.VMEM((2 * rows, JC), F32),
            pltpu.VMEM((2 * rows, 2 * hw), BF16),
            pltpu.VMEM((nc, 2, side, 2, br, ow), F32),
            pltpu.VMEM((nc, 2, side, 2, br, ow), BF16),
            pltpu.VMEM((nc, 2, 2, br, ow), BF16),
            pltpu.VMEM((nc, 2, 2, 2, br, ow), BF16),
            pltpu.VMEM((nc, 2, side, 2, qr, qc), F32),
            pltpu.VMEM((nc, 2, side, 2, qr, qc), BF16),
            pltpu.VMEM((nc, 2, 2, qr, qc), BF16),
            pltpu.VMEM((nc, 2, 2, 2, qr, qc), BF16),
            pltpu.VMEM((nc, 2, qr, qc), BF16),
            pltpu.VMEM((2, rows, cols), BF16),
            dma((nk,)), dma, dma((nk,)), dma((SLOTS, 2)), dma((nc,)), dma, dma((nj,)), dma,
            dma, dma, dma, dma, dma, dma, dma, dma, dma,
            dma((nc, 2, 2)), dma((nc, 2, 2, 2)), dma((nc, 2, 2)), dma((nc, 2, 2, 2)), dma((nc, 2)),
            dma((nc, 2, 2, 2)), dma((nc, 2, 2, 2)),
        ]
        any_spec = pl.BlockSpec(memory_space=pl.ANY)
        return pl.pallas_call(
            functools.partial(kernel, side),
            out_shape=jax.ShapeDtypeStruct((rows, 2 * cols), BF16),
            in_specs=[any_spec] * 4,
            out_specs=any_spec,
            scratch_shapes=scratch,
            compiler_params=pltpu.CompilerParams(
                collective_id=0, has_side_effects=True, vmem_limit_bytes=67_043_328
            ),
            cost_estimate=pl.CostEstimate(
                flops=6 * rows * depth * 2 * hw, bytes_accessed=6 * depth * hw, transcendentals=2 * rows * hw
            ),
        )(x, w_gate, w_up, w_down)

    return jax.shard_map(
        step,
        mesh=mesh,
        in_specs=(P("dp", None), P(None, "tp"), P(None, "tp"), P("tp", None)),
        out_specs=P("dp", None),
        check_vma=False,
    )
```

time: 139 us -> 68.5 us (0.49)
  waiting for transfers between devices: 83.1 us -> 0 us
  Pallas kernels: 0 us -> 65.3 us
  matrix products: 37.4 us -> 0 us
  between operations: 13.4 us -> 0.01 us
  local copies, waits for them, and re-layouts: 4.68 us -> 3.1 us
    psum x1 -> x0, waiting for transfers between devices: 83.1 us -> none  [step(): return lax.psum(term, 'tp')]
    pallas_call x0 -> x1, Pallas kernels: none -> 65.3 us  [step(): pl.pallas_call(functools.partial(kernel, side), out_shape=jax.ShapeDtypeS...]
    dot_general x2 -> x0, matrix products: 37.4 us -> none  [the longest x1 24.5 us: step(): jnp.dot(hidden, w_down, preferred_element_type=jnp.float32)]
    unnamed x3 -> x1, local copies, waits for them, and re-layouts: 4.68 us -> 3.1 us
  transfers between devices with their start and end apart: 1 -> 0, of which waited for: 1 -> 0; matrix products, arithmetic and copies ran while one was open for 0% -> 0% of each run, Pallas kernels for 0% -> 0%
where the time goes in v1:
time: 68.5 us; the launch traced here: 68.4 us
  Pallas kernels  65.3 us (95%)
  local copies, waits for them, and re-layouts  3.1 us (5%)
    pallas_call x1, Pallas kernels, step(): pl.pallas_call(functools.partial(kernel, side), out_shape=jax.ShapeDtypeS...  65.3 us
    unnamed x1, local copies, waits for them, and re-layouts  3.1 us

profile of v1, /device:TPU:96, one launch (start us, length us, event | category | flops | bytes accessed | tf_op | source)
XLA Modules:
  0.0 68.4 jit_solution(9111281634563814264)
XLA Ops:
  0.0 65.3 %shard_map.46 = bf16[128,8192]{1,0:T(8,128)(2,1)} custom-call(bf16[128,8192]{1,0:T(8,128)(2,1)} %x_ref.1, bf16[8192,2048]{1,0:T(8,128)(2,1)} %wg_ref.1, bf16[8192,2048]{1,0:T(8,128)(2,1)} %wu_ref.1, bf16[2048,8192]{1,0:T(8,128)(2,1)} %wd_ref.1), custom_call_target="tpu_custom_call" | custom-call | flops 12884901888 | bytes 50331648 | tf_op jit(solution)/shard_map/pallas_call | solution.py:329
  65.3 3.1 %copy.6 = bf16[128,8192]{1,0:T(8,128)(2,1)} copy(bf16[128,8192]{1,0:T(8,128)(2,1)} %shard_map.46) | data formatting | bytes 4194304

commit v2 on v1

--- a/solution.py
+++ b/solution.py
@@ -15,15 +15,16 @@
 JC = 512
 CW = 512
 SLOTS = 8
-LAG = 3
+RING_1 = True
+RING_2 = True
+LAG = 4
 
 
 def kernel(
     side, x_ref, wg_ref, wu_ref, wd_ref, out_ref,
-    xs, wgb, wub, wdb, accg, accu, hid, term, termb, r1, f1, red, redb, r2, f2, swp, ybuf,
+    xs, wgb, wub, wdb, accg, accu, hid, term, termb, f1, red, redb, f2, swp, ybuf,
     x_in, x_out, x_recv, w_in, wd_in, h_out, h_recv, y_out,
-    s_r1, s_f1, s_r2, s_f2, s_sw, s_g1, s_g1f, s_g2, s_g2f,
-    q_r1, q_f1, q_r2, q_f2, q_sw, q_g1, q_g2,
+    s_f1, s_f2, s_sw, s_g1, s_g2, q_f1, q_f2, q_sw, q_g1, q_g2,
 ):
     rows, depth = x_ref.shape
     hw = wg_ref.shape[1] // 2
@@ -44,7 +45,7 @@
             return (dp, lax.rem(cx + d + side, side) * side + cy)
         return (dp, cx * side + lax.rem(cy + d + side, side))
 
-    nbr = [[near(axis, 1), near(axis, -1)] for axis in (0, 1)]
+    nbr = [[near(axis, d) for d in (1, -1, 2)] for axis in (0, 1)]
     coord = [cx, cy]
 
     def send(src, dst, s_sem, r_sem, dev):
@@ -88,7 +89,7 @@
     barrier = pltpu.get_barrier_semaphore()
     for dev in (partner, *nbr[0], *nbr[1]):
         pl.semaphore_signal(barrier, inc=1, device_id=dev, device_id_type=MESH)
-    pl.semaphore_wait(barrier, 5)
+    pl.semaphore_wait(barrier, 7)
 
     for k in range(nk):
         x_piece(k).wait()
@@ -147,23 +148,15 @@
         q = pl.ds(pl.multiple_of(c * CW + o * ow, ow), ow)
         return r, q
 
-    def scatter_start(src, relay, fin, s_relay, s_fin, q_relay, q_fin, pos, dev):
-        send(src.at[wrap(pos + 2), 0], relay.at[0], s_relay, q_relay.at[0], dev[0]).start()
-        send(src.at[wrap(pos + 2), 1], relay.at[1], s_relay, q_relay.at[1], dev[1]).start()
-        send(src.at[wrap(pos + 1), 1], fin.at[0, 1], s_fin, q_fin.at[0, 1], dev[0]).start()
-        send(src.at[wrap(pos - 1), 0], fin.at[1, 0], s_fin, q_fin.at[1, 0], dev[1]).start()
-
-    def scatter_relay(own, relay, fin, s_fin, q_relay, q_fin, pos, dev):
+    def scatter_direct(src, fin, s_fin, sem, pos, dev):
+        for d, delta in enumerate((1, -1, 2)):
+            send(src.at[wrap(pos + delta)], fin.at[d], s_fin, sem(d), dev[d]).start()
+
+    def scatter_ring(src, fin, s_fin, q_fin, pos, dev):
         for d in (0, 1):
-            landed(relay.at[d], q_relay.at[d])
-            q = wrap(pos + 1 - 2 * d)
-            relay[d] = (relay[d].astype(F32) + own[q, d]).astype(BF16)
-            send(relay.at[d], fin.at[d, d], s_fin, q_fin.at[d, d], dev[d]).start()
-
-    def scatter_wait(fin, q_fin):
+            send(src.at[wrap(pos + 2), d], fin.at[2, d], s_fin, q_fin.at[2, d], dev[d]).start()
         for d in (0, 1):
-            for g in (0, 1):
-                landed(fin.at[d, g], q_fin.at[d, g])
+            send(src.at[wrap(pos + 1 - 2 * d), 1 - d], fin.at[d, 1 - d], s_fin, q_fin.at[d, 1 - d], dev[d]).start()
 
     def make_term(c):
         wd_block(c).wait()
@@ -175,44 +168,51 @@
                     term[c, o, q, g] = v
                     termb[c, o, q, g] = v.astype(BF16)
         for o in (0, 1):
-            scatter_start(
-                termb.at[c, o], r1.at[c, o], f1.at[c, o], s_r1, s_f1, q_r1.at[c, o], q_f1.at[c, o], coord[o], nbr[o]
-            )
+            if RING_1:
+                scatter_ring(termb.at[c, o], f1.at[c, o], s_f1, q_f1.at[c, o], coord[o], nbr[o])
+            else:
+                scatter_direct(
+                    termb.at[c, o], f1.at[c, o], s_f1, lambda d, o=o: q_f1.at[c, o, d, 0], coord[o], nbr[o]
+                )
 
     def relay_1(c):
         for o in (0, 1):
-            scatter_relay(
-                term.at[c, o], r1.at[c, o], f1.at[c, o], s_f1, q_r1.at[c, o], q_f1.at[c, o], coord[o], nbr[o]
-            )
+            for d in (0, 1):
+                part = f1.at[c, o, 2, d]
+                landed(part, q_f1.at[c, o, 2, d])
+                part[...] = (part[...].astype(F32) + term[c, o, wrap(coord[o] + 1 - 2 * d), d]).astype(BF16)
+                send(part, f1.at[c, o, d, d], s_f1, q_f1.at[c, o, d, d], nbr[o][d]).start()
 
     def reduce_1(c):
         for o in (0, 1):
-            scatter_wait(f1.at[c, o], q_f1.at[c, o])
+            if RING_1:
+                for d in (0, 1):
+                    for g in (0, 1):
+                        landed(f1.at[c, o, d, g], q_f1.at[c, o, d, g])
+            else:
+                for d in range(3):
+                    landed(f1.at[c, o, d], q_f1.at[c, o, d, 0])
             for g in (0, 1):
                 v = term[c, o, coord[o], g] + f1[c, o, 0, g].astype(F32) + f1[c, o, 1, g].astype(F32)
+                if not RING_1:
+                    v = v + f1[c, o, 2, g].astype(F32)
                 for q in range(side):
                     w = v[(q // 2) * qr:(q // 2 + 1) * qr, (q % 2) * qc:(q % 2 + 1) * qc]
                     red[c, o, q, g] = w
                     redb[c, o, q, g] = w.astype(BF16)
-            scatter_start(
-                redb.at[c, o], r2.at[c, o], f2.at[c, o], s_r2, s_f2, q_r2.at[c, o], q_f2.at[c, o],
-                coord[1 - o], nbr[1 - o],
+            scatter_direct(
+                redb.at[c, o], f2.at[c, o], s_f2, lambda d, o=o: q_f2.at[c, o, d], coord[1 - o], nbr[1 - o]
             )
 
-    def relay_2(c):
-        for o in (0, 1):
-            scatter_relay(
-                red.at[c, o], r2.at[c, o], f2.at[c, o], s_f2, q_r2.at[c, o], q_f2.at[c, o], coord[1 - o], nbr[1 - o]
-            )
-
     def reduce_2(c):
         for o in (0, 1):
-            scatter_wait(f2.at[c, o], q_f2.at[c, o])
             b = coord[1 - o]
+            for d in range(3):
+                landed(f2.at[c, o, d], q_f2.at[c, o, d])
 
             def total(g):
                 v = red[c, o, b, g] + f2[c, o, 0, g].astype(F32) + f2[c, o, 1, g].astype(F32)
-                return v.astype(BF16)
+                return (v + f2[c, o, 2, g].astype(F32)).astype(BF16)
 
             r, q = piece(c, o, b)
             swp[c, o] = total(other)
@@ -223,37 +223,35 @@
         for o in (0, 1):
             r, q = piece(c, o, coord[1 - o])
             landed(ybuf.at[other, r, q], q_sw.at[c, o])
-            for d in (0, 1):
-                send(ybuf.at[:, r, q], ybuf.at[:, r, q], s_g1, q_g1.at[c, o, 0, d], nbr[1 - o][d]).start()
-
-    def forward_1(c):
-        for o in (0, 1):
-            for d in (0, 1):
-                r, q = piece(c, o, wrap(coord[1 - o] - 1 + 2 * d))
-                landed(ybuf.at[:, r, q], q_g1.at[c, o, 0, d])
-                send(ybuf.at[d, r, q], ybuf.at[d, r, q], s_g1f, q_g1.at[c, o, 1, d], nbr[1 - o][d]).start()
+            for d in range(3):
+                send(ybuf.at[:, r, q], ybuf.at[:, r, q], s_g1, q_g1.at[c, o, d], nbr[1 - o][d]).start()
 
     def gather_2(c):
         for o in (0, 1):
-            r, q = piece(c, o, wrap(coord[1 - o] + 2))
-            for d in (0, 1):
-                landed(ybuf.at[d, r, q], q_g1.at[c, o, 1, d])
+            for d, delta in enumerate((-1, 1, 2)):
+                r, q = piece(c, o, wrap(coord[1 - o] + delta))
+                landed(ybuf.at[:, r, q], q_g1.at[c, o, d])
             r, q = slab(c, o, coord[o])
-            for d in (0, 1):
-                send(ybuf.at[:, r, q], ybuf.at[:, r, q], s_g2, q_g2.at[c, o, 0, d], nbr[o][d]).start()
+            for d in range(2 if RING_2 else 3):
+                send(ybuf.at[:, r, q], ybuf.at[:, r, q], s_g2, q_g2.at[c, o, d % 2, d // 2], nbr[o][d]).start()
 
     def forward_2(c):
         for o in (0, 1):
             for d in (0, 1):
                 r, q = slab(c, o, wrap(coord[o] - 1 + 2 * d))
-                landed(ybuf.at[:, r, q], q_g2.at[c, o, 0, d])
-                send(ybuf.at[d, r, q], ybuf.at[d, r, q], s_g2f, q_g2.at[c, o, 1, d], nbr[o][d]).start()
+                landed(ybuf.at[:, r, q], q_g2.at[c, o, d, 0])
+                send(ybuf.at[d, r, q], ybuf.at[d, r, q], s_g2, q_g2.at[c, o, d, 1], nbr[o][d]).start()
 
     def finish(c):
         for o in (0, 1):
-            r, q = slab(c, o, wrap(coord[o] + 2))
-            for d in (0, 1):
-                landed(ybuf.at[d, r, q], q_g2.at[c, o, 1, d])
+            if RING_2:
+                r, q = slab(c, o, wrap(coord[o] + 2))
+                for d in (0, 1):
+                    landed(ybuf.at[d, r, q], q_g2.at[c, o, d, 1])
+            else:
+                for d, delta in enumerate((-1, 1, 2)):
+                    r, q = slab(c, o, wrap(coord[o] + delta))
+                    landed(ybuf.at[:, r, q], q_g2.at[c, o, d % 2, d // 2])
         for d in (0, 1):
             pltpu.make_async_copy(
                 ybuf.at[d, :, pl.ds(pl.multiple_of(c * CW, CW), CW)],
@@ -261,9 +259,7 @@
                 y_out,
             ).start()
 
-    stages = (
-        make_term, relay_1, reduce_1, relay_2, reduce_2, gather_1, forward_1, gather_2, forward_2, finish,
-    )
+    stages = [make_term] + [relay_1] * RING_1 + [reduce_1, reduce_2, gather_1, gather_2] + [forward_2] * RING_2 + [finish]
 
     def tick(t, carry):
         for s, stage in enumerate(stages):
@@ -279,15 +275,11 @@
 
     left_device(ybuf, x_out)
     left_device(hid.at[:, pl.ds(0, hw)], h_out)
-    left_device(r1, s_r1)
     left_device(f1, s_f1)
-    left_device(r2, s_r2)
     left_device(f2, s_f2)
     left_device(swp, s_sw)
     left_device(f2, s_g1)
-    left_device(r2, s_g1f)
     left_device(f1, s_g2)
-    left_device(r1, s_g2f)
     pltpu.make_async_copy(ybuf, ybuf, y_out).wait()
 
 
@@ -312,18 +304,15 @@
             pltpu.VMEM((2 * rows, 2 * hw), BF16),
             pltpu.VMEM((nc, 2, side, 2, br, ow), F32),
             pltpu.VMEM((nc, 2, side, 2, br, ow), BF16),
-            pltpu.VMEM((nc, 2, 2, br, ow), BF16),
-            pltpu.VMEM((nc, 2, 2, 2, br, ow), BF16),
+            pltpu.VMEM((nc, 2, 3, 2, br, ow), BF16),
             pltpu.VMEM((nc, 2, side, 2, qr, qc), F32),
             pltpu.VMEM((nc, 2, side, 2, qr, qc), BF16),
-            pltpu.VMEM((nc, 2, 2, qr, qc), BF16),
-            pltpu.VMEM((nc, 2, 2, 2, qr, qc), BF16),
+            pltpu.VMEM((nc, 2, 3, 2, qr, qc), BF16),
             pltpu.VMEM((nc, 2, qr, qc), BF16),
             pltpu.VMEM((2, rows, cols), BF16),
             dma((nk,)), dma, dma((nk,)), dma((SLOTS, 2)), dma((nc,)), dma, dma((nj,)), dma,
-            dma, dma, dma, dma, dma, dma, dma, dma, dma,
-            dma((nc, 2, 2)), dma((nc, 2, 2, 2)), dma((nc, 2, 2)), dma((nc, 2, 2, 2)), dma((nc, 2)),
-            dma((nc, 2, 2, 2)), dma((nc, 2, 2, 2)),
+            dma, dma, dma, dma, dma,
+            dma((nc, 2, 3, 2)), dma((nc, 2, 3)), dma((nc, 2)), dma((nc, 2, 3)), dma((nc, 2, 2, 2)),
         ]
         any_spec = pl.BlockSpec(memory_space=pl.ANY)
         return pl.pallas_call(

time: 68.5 us -> 62.4 us (0.911)
  Pallas kernels: 65.3 us -> 59.2 us
    pallas_call x1, Pallas kernels: 65.3 us -> 59.2 us  [step(): pl.pallas_call(functools.partial(kernel, side), out_shape=jax.ShapeDtypeS...]
where the time goes in v2:
time: 62.4 us; the launch traced here: 62.3 us
  Pallas kernels  59.2 us (95%)
  local copies, waits for them, and re-layouts  3.1 us (5%)
    pallas_call x1, Pallas kernels, step(): pl.pallas_call(functools.partial(kernel, side), out_shape=jax.ShapeDtypeS...  59.2 us
    unnamed x1, local copies, waits for them, and re-layouts  3.1 us

profile of v2, /device:TPU:96, one launch (start us, length us, event | category | flops | bytes accessed | tf_op | source)
XLA Modules:
  0.0 62.3 jit_solution(10713138285684486504)
XLA Ops:
  0.0 59.2 %shard_map.46 = bf16[128,8192]{1,0:T(8,128)(2,1)} custom-call(bf16[128,8192]{1,0:T(8,128)(2,1)} %x_ref.1, bf16[8192,2048]{1,0:T(8,128)(2,1)} %wg_ref.1, bf16[8192,2048]{1,0:T(8,128)(2,1)} %wu_ref.1, bf16[2048,8192]{1,0:T(8,128)(2,1)} %wd_ref.1), custom_call_target="tpu_custom_call" | custom-call | flops 12884901888 | bytes 50331648 | tf_op jit(solution)/shard_map/pallas_call | solution.py:318
  59.2 3.1 %copy.6 = bf16[128,8192]{1,0:T(8,128)(2,1)} copy(bf16[128,8192]{1,0:T(8,128)(2,1)} %shard_map.46) | data formatting | bytes 4194304

commit v3 on v2

--- a/solution.py
+++ b/solution.py
@@ -11,24 +11,27 @@
 MESH = pl.DeviceIdType.MESH
 F32, BF16 = jnp.float32, jnp.bfloat16
 
+VMEM_LIMIT = 51 << 20
 KC = 1024
 JC = 512
 CW = 512
-SLOTS = 8
+FIRST = 2
+DEPTH = 6
+AHEAD = 4
 RING_1 = True
 RING_2 = True
 LAG = 4
 
 
 def kernel(
-    side, x_ref, wg_ref, wu_ref, wd_ref, out_ref,
-    xs, wgb, wub, wdb, accg, accu, hid, term, termb, f1, red, redb, f2, swp, ybuf,
-    x_in, x_out, x_recv, w_in, wd_in, h_out, h_recv, y_out,
+    side, x_ref, wg_ref, wu_ref, wd_ref, ybuf,
+    xs, pool, acc, hid, term, termb, f1, red, redb, f2, swp,
+    x_in, x_out, x_recv, w_in, wd_in, h_out, h_recv,
     s_f1, s_f2, s_sw, s_g1, s_g2, q_f1, q_f2, q_sw, q_g1, q_g2,
 ):
     rows, depth = x_ref.shape
     hw = wg_ref.shape[1] // 2
-    cols = out_ref.shape[1] // 2
+    cols = ybuf.shape[2]
     nk, nj, nc = depth // KC, hw // JC, cols // CW
     nblk = nk * nj
     ow = CW // 2
@@ -68,71 +71,130 @@
         return pltpu.make_async_copy(x_ref.at[:, c], xs.at[h, :, c], x_in.at[k])
 
     def w_block(i):
-        j, k, slot = i // nk, lax.rem(i, nk), lax.rem(i, SLOTS)
+        j, k = i // nk, lax.rem(i, nk)
         r = pl.ds(pl.multiple_of(k * KC, KC), KC)
         c = pl.ds(pl.multiple_of(h * hw + j * JC, JC), JC)
-        return (
-            pltpu.make_async_copy(wg_ref.at[r, c], wgb.at[slot], w_in.at[slot, 0]),
-            pltpu.make_async_copy(wu_ref.at[r, c], wub.at[slot], w_in.at[slot, 1]),
-        )
+        return [
+            pltpu.make_async_copy(ref.at[r, c], pool.at[i, m], w_in.at[i, m]) for m, ref in enumerate((wg_ref, wu_ref))
+        ]
 
     def wd_block(c):
         cc = pl.ds(pl.multiple_of(h * cols + c * CW, CW), CW)
-        return pltpu.make_async_copy(wd_ref.at[:, cc], wdb.at[c], wd_in.at[c])
-
-    for k in range(nk):
-        x_piece(k).start()
-    for i in range(SLOTS):
-        for cp in w_block(i):
+        return [
+            pltpu.make_async_copy(wd_ref.at[pl.ds(m * hw, hw), cc], pool.at[c, m], wd_in.at[c, m]) for m in (0, 1)
+        ]
+
+    def wait_all(copies):
+        for cp in copies:
+            cp.wait()
+
+    def start_all(copies):
+        for cp in copies:
             cp.start()
 
     barrier = pltpu.get_barrier_semaphore()
     for dev in (partner, *nbr[0], *nbr[1]):
         pl.semaphore_signal(barrier, inc=1, device_id=dev, device_id_type=MESH)
+
+    for k in range(nk):
+        x_piece(k).start()
+    for i in range(FIRST):
+        start_all(w_block(i))
+    acc[...] = jnp.zeros_like(acc)
+
+    def chunk_of_x(k):
+        return pl.ds(pl.multiple_of(k * KC, KC), KC)
+
+    def following(i):
+        @pl.when(i < nblk)
+        def _():
+            start_all(w_block(i))
+
+        @pl.when(i >= nblk)
+        def _():
+            start_all(wd_block(i - nblk))
+
+    def all_rows(j, k):
+        wait_all(w_block(j * nk + k))
+        following(j * nk + k + DEPTH)
+        lhs = xs[:, :, chunk_of_x(k)].reshape(2 * rows, KC)
+        for m in (0, 1):
+            acc[j, m] += jnp.dot(lhs, pool[j * nk + k, m], preferred_element_type=F32).reshape(2, rows, JC)
+
+    def send_hidden(j, n, width):
+        c = pl.ds(pl.multiple_of(h * hw + j * JC + n * width, width), width)
+        send(hid.at[:, c], hid.at[:, c], h_out, h_recv.at[j + n], partner).start()
+
     pl.semaphore_wait(barrier, 7)
-
     for k in range(nk):
         x_piece(k).wait()
         c = pl.ds(k * KC, KC)
         send(xs.at[h, :, c], xs.at[h, :, c], x_out, x_recv.at[k], partner).start()
-
-    for j in range(nj):
-        accg[...] = jnp.zeros_like(accg)
-        accu[...] = jnp.zeros_like(accu)
-
-        def block(k, carry, j=j):
-            i = j * nk + k
-            slot = lax.rem(i, SLOTS)
-            kc = pl.ds(pl.multiple_of(k * KC, KC), KC)
-            if j == 0:
-                landed(xs.at[other, :, kc], x_recv.at[k])
-            for cp in w_block(i):
-                cp.wait()
-            lhs = xs[:, :, kc].reshape(2 * rows, KC)
-            accg[...] += jnp.dot(lhs, wgb[slot], preferred_element_type=F32)
-            accu[...] += jnp.dot(lhs, wub[slot], preferred_element_type=F32)
-
-            @pl.when(i + SLOTS < nblk)
-            def _():
-                for cp in w_block(i + SLOTS):
-                    cp.start()
-
-            @pl.when((i + SLOTS >= nblk) & (i + SLOTS < nblk + nc))
-            def _():
-                wd_block(i + SLOTS - nblk).start()
-
-            return carry
-
-        lax.fori_loop(0, nk, block, 0)
-        g = accg[...]
-        hc = pl.ds(pl.multiple_of(h * hw + j * JC, JC), JC)
-        hid[:, hc] = (jax.nn.silu(g) * accu[...]).astype(BF16)
-        send(hid.at[:, hc], hid.at[:, hc], h_out, h_recv.at[j], partner).start()
-    for c in range(SLOTS, nc):
-        wd_block(c).start()
-    for j in range(nj):
-        hc = pl.ds(pl.multiple_of(other * hw + j * JC, JC), JC)
-        landed(hid.at[:, hc], h_recv.at[j])
+    for i in range(FIRST, DEPTH):
+        start_all(w_block(i))
+
+    def first_half(k, carry):
+        landed(xs.at[other, :, chunk_of_x(k)], x_recv.at[k])
+        all_rows(0, k)
+        return carry
+
+    lax.fori_loop(0, nk, first_half, 0)
+
+    def with_act(t, carry):
+        all_rows(1, t)
+        hc = pl.ds(pl.multiple_of(h * hw, JC), JC)
+        hid[pl.ds(pl.multiple_of(t * rows, rows), rows), hc] = (
+            jax.nn.silu(acc[0, 0, t]) * acc[0, 1, t]
+        ).astype(BF16)
+        return carry
+
+    lax.fori_loop(0, 2, with_act, 0)
+    send_hidden(0, 0, JC)
+
+    def second_half(k, carry):
+        all_rows(1, k)
+        return carry
+
+    lax.fori_loop(2, nk - 1, second_half, 0)
+    k = nk - 1
+    wait_all(w_block(nk + k))
+    following(nk + k + DEPTH)
+    lhs = xs[:, :, chunk_of_x(k)].reshape(2 * rows, KC)
+    half = JC // 2
+    for n in (0, 1):
+        cc = slice(n * half, (n + 1) * half)
+        g, u = (
+            acc[1, m, :, :, cc].reshape(2 * rows, half)
+            + jnp.dot(lhs, pool[nk + k, m, :, cc], preferred_element_type=F32)
+            for m in (0, 1)
+        )
+        hid[:, pl.ds(pl.multiple_of(h * hw + JC + n * half, half), half)] = (jax.nn.silu(g) * u).astype(BF16)
+        send_hidden(1, n, half)
+
+    mine = pl.ds(pl.multiple_of(h * hw, hw), hw)
+    theirs = pl.ds(pl.multiple_of(other * hw, hw), hw)
+
+    def own_half(c):
+        wait_all(wd_block(c))
+
+        @pl.when(c + DEPTH < nc)
+        def _():
+            start_all(wd_block(c + DEPTH))
+
+        t = jnp.dot(hid[:, mine], pool[c, h], preferred_element_type=F32)
+        for o in (0, 1):
+            for q in range(side):
+                for g in (0, 1):
+                    term[c, o, q, g] = t[g * rows + q * br:g * rows + (q + 1) * br, o * ow:(o + 1) * ow]
+
+    def ahead(c, carry):
+        own_half(c)
+        return carry
+
+    lax.fori_loop(0, AHEAD, ahead, 0)
+    for j, n, width in ((0, 0, JC), (1, 0, half), (1, 1, half)):
+        c = pl.ds(pl.multiple_of(other * hw + j * JC + n * width, width), width)
+        landed(hid.at[:, c], h_recv.at[j + n])
 
     def wrap(v):
         return lax.rem(v + 2 * side, side)
@@ -159,12 +221,12 @@
             send(src.at[wrap(pos + 1 - 2 * d), 1 - d], fin.at[d, 1 - d], s_fin, q_fin.at[d, 1 - d], dev[d]).start()
 
     def make_term(c):
-        wd_block(c).wait()
-        t = jnp.dot(hid[...], wdb[c], preferred_element_type=F32)
+        t = jnp.dot(hid[:, theirs], pool[c, other], preferred_element_type=F32)
         for o in (0, 1):
             for q in range(side):
                 for g in (0, 1):
                     v = t[g * rows + q * br:g * rows + (q + 1) * br, o * ow:(o + 1) * ow]
+                    v = v + term[c, o, q, g]
                     term[c, o, q, g] = v
                     termb[c, o, q, g] = v.astype(BF16)
         for o in (0, 1):
@@ -174,6 +236,10 @@
                 scatter_direct(
                     termb.at[c, o], f1.at[c, o], s_f1, lambda d, o=o: q_f1.at[c, o, d, 0], coord[o], nbr[o]
                 )
+
+        @pl.when(c + AHEAD < nc)
+        def _():
+            own_half(c + AHEAD)
 
     def relay_1(c):
         for o in (0, 1):
@@ -252,12 +318,6 @@
                 for d, delta in enumerate((-1, 1, 2)):
                     r, q = slab(c, o, wrap(coord[o] + delta))
                     landed(ybuf.at[:, r, q], q_g2.at[c, o, d % 2, d // 2])
-        for d in (0, 1):
-            pltpu.make_async_copy(
-                ybuf.at[d, :, pl.ds(pl.multiple_of(c * CW, CW), CW)],
-                out_ref.at[:, pl.ds(pl.multiple_of(d * cols + c * CW, CW), CW)],
-                y_out,
-            ).start()
 
     stages = [make_term] + [relay_1] * RING_1 + [reduce_1, reduce_2, gather_1, gather_2] + [forward_2] * RING_2 + [finish]
 
@@ -280,7 +340,24 @@
     left_device(swp, s_sw)
     left_device(f2, s_g1)
     left_device(f1, s_g2)
-    pltpu.make_async_copy(ybuf, ybuf, y_out).wait()
+
+
+def write_out(y_ref, out_ref, sem):
+    rows, cols = y_ref.shape[1:]
+    n = sem.shape[1]
+    copies = [
+        pltpu.make_async_copy(
+            y_ref.at[d, pl.ds(i * rows // n, rows // n)],
+            out_ref.at[pl.ds(i * rows // n, rows // n), pl.ds(d * cols, cols)],
+            sem.at[d, i],
+        )
+        for d in (0, 1)
+        for i in range(n)
+    ]
+    for cp in copies:
+        cp.start()
+    for cp in copies:
+        cp.wait()
 
 
 def solution(mesh):
@@ -296,11 +373,8 @@
         dma = pltpu.SemaphoreType.DMA
         scratch = [
             pltpu.VMEM((2, rows, depth), BF16),
-            pltpu.VMEM((SLOTS, KC, JC), BF16),
-            pltpu.VMEM((SLOTS, KC, JC), BF16),
-            pltpu.VMEM((nc, 2 * hw, CW), BF16),
-            pltpu.VMEM((2 * rows, JC), F32),
-            pltpu.VMEM((2 * rows, JC), F32),
+            pltpu.VMEM((nk * nj, 2, KC, JC), BF16),
+            pltpu.VMEM((nj, 2, 2, rows, JC), F32),
             pltpu.VMEM((2 * rows, 2 * hw), BF16),
             pltpu.VMEM((nc, 2, side, 2, br, ow), F32),
             pltpu.VMEM((nc, 2, side, 2, br, ow), BF16),
@@ -309,25 +383,32 @@
             pltpu.VMEM((nc, 2, side, 2, qr, qc), BF16),
             pltpu.VMEM((nc, 2, 3, 2, qr, qc), BF16),
             pltpu.VMEM((nc, 2, qr, qc), BF16),
-            pltpu.VMEM((2, rows, cols), BF16),
-            dma((nk,)), dma, dma((nk,)), dma((SLOTS, 2)), dma((nc,)), dma, dma((nj,)), dma,
+            dma((nk,)), dma, dma((nk,)), dma((nk * nj, 2)), dma((nc, 2)), dma, dma((nj + 1,)),
             dma, dma, dma, dma, dma,
             dma((nc, 2, 3, 2)), dma((nc, 2, 3)), dma((nc, 2)), dma((nc, 2, 3)), dma((nc, 2, 2, 2)),
         ]
         any_spec = pl.BlockSpec(memory_space=pl.ANY)
-        return pl.pallas_call(
+        y = pl.pallas_call(
             functools.partial(kernel, side),
-            out_shape=jax.ShapeDtypeStruct((rows, 2 * cols), BF16),
+            out_shape=jax.ShapeDtypeStruct((2, rows, cols), BF16),
             in_specs=[any_spec] * 4,
-            out_specs=any_spec,
+            out_specs=pl.BlockSpec(memory_space=pltpu.VMEM),
             scratch_shapes=scratch,
             compiler_params=pltpu.CompilerParams(
-                collective_id=0, has_side_effects=True, vmem_limit_bytes=67_043_328
+                collective_id=0, has_side_effects=True, vmem_limit_bytes=VMEM_LIMIT
             ),
             cost_estimate=pl.CostEstimate(
                 flops=6 * rows * depth * 2 * hw, bytes_accessed=6 * depth * hw, transcendentals=2 * rows * hw
             ),
-        )(x, w_gate, w_up, w_down)
+        )(pltpu.with_memory_space_constraint(x, pltpu.HBM), w_gate, w_up, w_down)
+        return pl.pallas_call(
+            write_out,
+            out_shape=jax.ShapeDtypeStruct((rows, 2 * cols), BF16),
+            in_specs=[pl.BlockSpec(memory_space=pltpu.VMEM)],
+            out_specs=any_spec,
+            scratch_shapes=[dma((2, 4))],
+            compiler_params=pltpu.CompilerParams(vmem_limit_bytes=1 << 20),
+        )(y)
 
     return jax.shard_map(
         step,

time: 62.4 us -> 58.2 us (0.933)
  local copies, waits for them, and re-layouts: 3.1 us -> 0 us
  Pallas kernels: 59.2 us -> 58.1 us
    unnamed x1 -> x0, local copies, waits for them, and re-layouts: 3.1 us -> none
    pallas_call x1, Pallas kernels: 59.2 us -> 56.7 us  [step(): pl.pallas_call(functools.partial(kernel, side), out_shape=jax.ShapeDtypeS...]
    pallas_call x0 -> x1, Pallas kernels: none -> 1.38 us  [step(): pl.pallas_call(write_out, out_shape=jax.ShapeDtypeStruct((rows, 2 * cols)...]
where the time goes in v3:
time: 58.2 us; the launch traced here: 58.1 us
  Pallas kernels  58.1 us (100%)
    pallas_call x1, Pallas kernels, step(): pl.pallas_call(functools.partial(kernel, side), out_shape=jax.ShapeDtypeS...  56.7 us
    pallas_call x1, Pallas kernels, step(): pl.pallas_call(write_out, out_shape=jax.ShapeDtypeStruct((rows, 2 * cols)...  1.38 us

profile of v3, /device:TPU:96, one launch (start us, length us, event | category | flops | bytes accessed | tf_op | source)
XLA Modules:
  0.0 58.1 jit_solution(15299286386897301746)
XLA Ops:
  0.0 56.7 %shard_map.46.y_ref = bf16[2,128,4096]{2,1,0:T(8,128)(2,1)S(1)} custom-call(bf16[128,8192]{1,0:T(8,128)(2,1)} %x_ref.1, bf16[8192,2048]{1,0:T(8,128)(2,1)} %wg_ref.1, bf16[8192,2048]{1,0:T(8,128)(2,1)} %wu_ref.1, bf16[2048,8192]{1,0:T(8,128)(2,1)} %wd_ref.1), custom_call_target="tpu_custom_call" | custom-call | flops 12884901888 | bytes 50331648 | tf_op jit(solution)/shard_map/pallas_call | solution.py:391
  56.7 1.4 %shard_map.47 = bf16[128,8192]{1,0:T(8,128)(2,1)} custom-call(bf16[2,128,4096]{2,1,0:T(8,128)(2,1)S(1)} %shard_map.46.y_ref), custom_call_target="tpu_custom_call" | custom-call | tf_op jit(solution)/shard_map/pallas_call | solution.py:404

commit v4 on v3

--- a/solution.py
+++ b/solution.py
@@ -17,10 +17,10 @@
 CW = 512
 FIRST = 2
 DEPTH = 6
-AHEAD = 4
-RING_1 = True
-RING_2 = True
-LAG = 4
+AHEAD = 2
+STRAIGHT_1 = 0
+STRAIGHT_2 = 2
+LAG = 6
 
 
 def kernel(
@@ -229,10 +229,14 @@
                     v = v + term[c, o, q, g]
                     term[c, o, q, g] = v
                     termb[c, o, q, g] = v.astype(BF16)
-        for o in (0, 1):
-            if RING_1:
+        @pl.when(c < nc - STRAIGHT_1)
+        def _():
+            for o in (0, 1):
                 scatter_ring(termb.at[c, o], f1.at[c, o], s_f1, q_f1.at[c, o], coord[o], nbr[o])
-            else:
+
+        @pl.when(c >= nc - STRAIGHT_1)
+        def _():
+            for o in (0, 1):
                 scatter_direct(
                     termb.at[c, o], f1.at[c, o], s_f1, lambda d, o=o: q_f1.at[c, o, d, 0], coord[o], nbr[o]
                 )
@@ -242,33 +246,41 @@
             own_half(c + AHEAD)
 
     def relay_1(c):
-        for o in (0, 1):
-            for d in (0, 1):
-                part = f1.at[c, o, 2, d]
-                landed(part, q_f1.at[c, o, 2, d])
-                part[...] = (part[...].astype(F32) + term[c, o, wrap(coord[o] + 1 - 2 * d), d]).astype(BF16)
-                send(part, f1.at[c, o, d, d], s_f1, q_f1.at[c, o, d, d], nbr[o][d]).start()
+        @pl.when(c < nc - STRAIGHT_1)
+        def _():
+            for o in (0, 1):
+                for d in (0, 1):
+                    part = f1.at[c, o, 2, d]
+                    landed(part, q_f1.at[c, o, 2, d])
+                    part[...] = (part[...].astype(F32) + term[c, o, wrap(coord[o] + 1 - 2 * d), d]).astype(BF16)
+                    send(part, f1.at[c, o, d, d], s_f1, q_f1.at[c, o, d, d], nbr[o][d]).start()
+
+    def split_slab(c, o, n):
+        for g in (0, 1):
+            v = term[c, o, coord[o], g]
+            for d in range(n):
+                v = v + f1[c, o, d, g].astype(F32)
+            for q in range(side):
+                w = v[(q // 2) * qr:(q // 2 + 1) * qr, (q % 2) * qc:(q % 2 + 1) * qc]
+                red[c, o, q, g] = w
+                redb[c, o, q, g] = w.astype(BF16)
+        scatter_direct(redb.at[c, o], f2.at[c, o], s_f2, lambda d: q_f2.at[c, o, d], coord[1 - o], nbr[1 - o])
 
     def reduce_1(c):
-        for o in (0, 1):
-            if RING_1:
+        @pl.when(c < nc - STRAIGHT_1)
+        def _():
+            for o in (0, 1):
                 for d in (0, 1):
                     for g in (0, 1):
                         landed(f1.at[c, o, d, g], q_f1.at[c, o, d, g])
-            else:
+                split_slab(c, o, 2)
+
+        @pl.when(c >= nc - STRAIGHT_1)
+        def _():
+            for o in (0, 1):
                 for d in range(3):
                     landed(f1.at[c, o, d], q_f1.at[c, o, d, 0])
-            for g in (0, 1):
-                v = term[c, o, coord[o], g] + f1[c, o, 0, g].astype(F32) + f1[c, o, 1, g].astype(F32)
-                if not RING_1:
-                    v = v + f1[c, o, 2, g].astype(F32)
-                for q in range(side):
-                    w = v[(q // 2) * qr:(q // 2 + 1) * qr, (q % 2) * qc:(q % 2 + 1) * qc]
-                    red[c, o, q, g] = w
-                    redb[c, o, q, g] = w.astype(BF16)
-            scatter_direct(
-                redb.at[c, o], f2.at[c, o], s_f2, lambda d, o=o: q_f2.at[c, o, d], coord[1 - o], nbr[1 - o]
-            )
+                split_slab(c, o, 3)
 
     def reduce_2(c):
         for o in (0, 1):
@@ -298,28 +310,38 @@
                 r, q = piece(c, o, wrap(coord[1 - o] + delta))
                 landed(ybuf.at[:, r, q], q_g1.at[c, o, d])
             r, q = slab(c, o, coord[o])
-            for d in range(2 if RING_2 else 3):
-                send(ybuf.at[:, r, q], ybuf.at[:, r, q], s_g2, q_g2.at[c, o, d % 2, d // 2], nbr[o][d]).start()
+            for d in (0, 1):
+                send(ybuf.at[:, r, q], ybuf.at[:, r, q], s_g2, q_g2.at[c, o, d, 0], nbr[o][d]).start()
+
+            @pl.when(c >= nc - STRAIGHT_2)
+            def _(o=o, r=r, q=q):
+                send(ybuf.at[:, r, q], ybuf.at[:, r, q], s_g2, q_g2.at[c, o, 0, 1], nbr[o][2]).start()
 
     def forward_2(c):
         for o in (0, 1):
             for d in (0, 1):
                 r, q = slab(c, o, wrap(coord[o] - 1 + 2 * d))
                 landed(ybuf.at[:, r, q], q_g2.at[c, o, d, 0])
-                send(ybuf.at[d, r, q], ybuf.at[d, r, q], s_g2, q_g2.at[c, o, d, 1], nbr[o][d]).start()
+
+                @pl.when(c < nc - STRAIGHT_2)
+                def _(o=o, d=d, r=r, q=q):
+                    send(ybuf.at[d, r, q], ybuf.at[d, r, q], s_g2, q_g2.at[c, o, d, 1], nbr[o][d]).start()
 
     def finish(c):
-        for o in (0, 1):
-            if RING_2:
+        @pl.when(c < nc - STRAIGHT_2)
+        def _():
+            for o in (0, 1):
                 r, q = slab(c, o, wrap(coord[o] + 2))
                 for d in (0, 1):
                     landed(ybuf.at[d, r, q], q_g2.at[c, o, d, 1])
-            else:
-                for d, delta in enumerate((-1, 1, 2)):
-                    r, q = slab(c, o, wrap(coord[o] + delta))
-                    landed(ybuf.at[:, r, q], q_g2.at[c, o, d % 2, d // 2])
-
-    stages = [make_term] + [relay_1] * RING_1 + [reduce_1, reduce_2, gather_1, gather_2] + [forward_2] * RING_2 + [finish]
+
+        @pl.when(c >= nc - STRAIGHT_2)
+        def _():
+            for o in (0, 1):
+                r, q = slab(c, o, wrap(coord[o] + 2))
+                landed(ybuf.at[:, r, q], q_g2.at[c, o, 0, 1])
+
+    stages = (make_term, relay_1, reduce_1, reduce_2, gather_1, gather_2, forward_2, finish)
 
     def tick(t, carry):
         for s, stage in enumerate(stages):

time: 58.2 us -> 57.7 us (level)
  no operation moved by 1% of the time
where the time goes in v4:
time: 57.7 us; the launch traced here: 57.6 us
  Pallas kernels  57.6 us (100%)
    pallas_call x1, Pallas kernels, step(): pl.pallas_call(functools.partial(kernel, side), out_shape=jax.ShapeDtypeS...  56.2 us
    pallas_call x1, Pallas kernels, step(): pl.pallas_call(write_out, out_shape=jax.ShapeDtypeStruct((rows, 2 * cols)...  1.38 us

profile of v4, /device:TPU:96, one launch (start us, length us, event | category | flops | bytes accessed | tf_op | source)
XLA Modules:
  0.0 57.6 jit_solution(1538498238547574042)
XLA Ops:
  0.0 56.2 %shard_map.46.y_ref = bf16[2,128,4096]{2,1,0:T(8,128)(2,1)S(1)} custom-call(bf16[128,8192]{1,0:T(8,128)(2,1)} %x_ref.1, bf16[8192,2048]{1,0:T(8,128)(2,1)} %wg_ref.1, bf16[8192,2048]{1,0:T(8,128)(2,1)} %wu_ref.1, bf16[2048,8192]{1,0:T(8,128)(2,1)} %wd_ref.1), custom_call_target="tpu_custom_call" | custom-call | flops 12884901888 | bytes 50331648 | tf_op jit(solution)/shard_map/pallas_call | solution.py:413
  56.2 1.4 %shard_map.47 = bf16[128,8192]{1,0:T(8,128)(2,1)} custom-call(bf16[2,128,4096]{2,1,0:T(8,128)(2,1)S(1)} %shard_map.46.y_ref), custom_call_target="tpu_custom_call" | custom-call | tf_op jit(solution)/shard_map/pallas_call | solution.py:426

commit v5 on v4

--- a/solution.py
+++ b/solution.py
@@ -19,8 +19,8 @@
 DEPTH = 6
 AHEAD = 2
 STRAIGHT_1 = 0
-STRAIGHT_2 = 2
-LAG = 6
+STRAIGHT_2 = 3
+LAG = 5
 
 
 def kernel(
@@ -138,7 +138,7 @@
         all_rows(0, k)
         return carry
 
-    lax.fori_loop(0, nk, first_half, 0)
+    lax.fori_loop(0, nk, first_half, 0, unroll=2)
 
     def with_act(t, carry):
         all_rows(1, t)
@@ -155,7 +155,7 @@
         all_rows(1, k)
         return carry
 
-    lax.fori_loop(2, nk - 1, second_half, 0)
+    lax.fori_loop(2, nk - 1, second_half, 0, unroll=True)
     k = nk - 1
     wait_all(w_block(nk + k))
     following(nk + k + DEPTH)

time: 57.7 us -> 56 us (0.971)
  Pallas kernels: 57.6 us -> 56 us
    pallas_call x1, Pallas kernels: 56.2 us -> 54.6 us  [step(): pl.pallas_call(functools.partial(kernel, side), out_shape=jax.ShapeDtypeS...]
where the time goes in v5:
time: 56 us
  Pallas kernels  56 us (100%)
    pallas_call x1, Pallas kernels, step(): pl.pallas_call(functools.partial(kernel, side), out_shape=jax.ShapeDtypeS...  54.6 us
    pallas_call x1, Pallas kernels, step(): pl.pallas_call(write_out, out_shape=jax.ShapeDtypeStruct((rows, 2 * cols)...  1.38 us

profile of v5, /device:TPU:96, one launch (start us, length us, event | category | flops | bytes accessed | tf_op | source)
XLA Modules:
  0.0 56.0 jit_solution(1427670936617595085)
XLA Ops:
  0.0 54.6 %shard_map.46.y_ref = bf16[2,128,4096]{2,1,0:T(8,128)(2,1)S(1)} custom-call(bf16[128,8192]{1,0:T(8,128)(2,1)} %x_ref.1, bf16[8192,2048]{1,0:T(8,128)(2,1)} %wg_ref.1, bf16[8192,2048]{1,0:T(8,128)(2,1)} %wu_ref.1, bf16[2048,8192]{1,0:T(8,128)(2,1)} %wd_ref.1), custom_call_target="tpu_custom_call" | custom-call | flops 12884901888 | bytes 50331648 | tf_op jit(solution)/shard_map/pallas_call | solution.py:413
  54.6 1.4 %shard_map.47 = bf16[128,8192]{1,0:T(8,128)(2,1)} custom-call(bf16[2,128,4096]{2,1,0:T(8,128)(2,1)S(1)} %shard_map.46.y_ref), custom_call_target="tpu_custom_call" | custom-call | tf_op jit(solution)/shard_map/pallas_call | solution.py:426
